TPU v7x, 128 devices: a whole 4x4x4 slice. The times are simulated.
128 devices in a mesh: row: 8 (over y, x_lo), col: 16 (over x_hi, z, core).
Axes of the slice: x: 4 (x_hi: 2, x_lo: 2; x = x_hi * 2 + x_lo), y: 4, z: 4, core: 2. Of those that a mesh axis runs over, the one named last changes fastest.
Arguments:
- u_field: float32 [256, 16384], P('row', 'col'), may hold values from -4 to 4
- v_field: float32 [256, 16384], P('row', 'col'), may hold values from -7.5 to 7.5
- stimulus: float32 [256, 16384], P('row', 'col'), may hold values from -6 to 6
Outputs:
- u_final: float32 [256, 16384], P('row', 'col')
- v_final: float32 [256, 16384], P('row', 'col')
All inputs are finite; a program needn't handle non-finite values.
Results may differ from a plain program's by a relative error of at most 0.0003.
Values sent between devices are 32-bit elements; how exact they have to be, the bound alone decides.
A program may use at most 64 MiB of HBM per device.

v0:
```python
import jax
import jax.numpy as jnp
from jax import lax
from jax.sharding import PartitionSpec as P

MICRO_COUNT = 4
MIDDLE = 3
TOP = 3
OUTER = 2


RATE_U = 0.125
RATE_V = 0.125
TIME_STEP = 0.05
RECOVERY = 0.08
OFFSET = 0.7
DAMPING = 0.8


def extended(block, sides, width):
    for axis, dim in sides:
        count = lax.axis_size(axis)
        forward = [(i, i + 1) for i in range(count - 1)]
        forward.append((count - 1, 0))
        backward = [(target, source) for source, target in forward]
        low = lax.ppermute(
            lax.slice_in_dim(block, block.shape[dim] - width, None, axis=dim), axis, forward
        )
        high = lax.ppermute(lax.slice_in_dim(block, 0, width, axis=dim), axis, backward)
        block = jnp.concatenate([low, block, high], axis=dim)
    return block


def advance(padded, stimulus):
    centre = padded[:, 1:-1, 1:-1]
    beside_all = padded[:, :-2, 1:-1] + padded[:, 2:, 1:-1]
    beside_all = beside_all + padded[:, 1:-1, :-2] + padded[:, 1:-1, 2:]
    beside_all = beside_all - 4.0 * centre
    u_now = centre[0]
    v_now = centre[1]
    u_next = (
        u_now
        + RATE_U * beside_all[0]
        + TIME_STEP * (u_now - u_now * u_now * u_now / 3.0 - v_now + stimulus)
    )
    v_next = (
        v_now + RATE_V * beside_all[1] + TIME_STEP * RECOVERY * (u_now + OFFSET - DAMPING * v_now)
    )
    return jnp.stack([u_next, v_next])


def forward_linear_jump(inner, repeats, fields):

    def turn(present_index, pair_now):
        return (pair_now[1], inner(pair_now[1]))

    previous_fields, latest = lax.fori_loop(0, repeats, turn, (fields, fields))
    return latest + (latest - previous_fields)


def body(u_field, v_field, stimulus):
    fields = jnp.stack([u_field, v_field])
    halo_width_total = MIDDLE * MICRO_COUNT
    stim_wide = extended(stimulus, (("row", 0), ("col", 1)), halo_width_total)
    height = stim_wide.shape[0]
    breadth = stim_wide.shape[1]

    def local_first(padded, depth):
        previous_fields = padded
        for telescope_advance_once in range(MICRO_COUNT):
            if telescope_advance_once == MICRO_COUNT - 1:
                previous_fields = padded[:, 1:-1, 1:-1]
            depth = depth - 1
            inset = halo_width_total - depth
            window = stim_wide[inset : height - inset, inset : breadth - inset]
            padded = advance(padded, window)
        return padded + (padded - previous_fields)

    def second(initial_fields_pair):
        padded = extended(initial_fields_pair, (("row", 1), ("col", 2)), halo_width_total)
        previous_fields = padded
        depth = halo_width_total
        for middle_step in range(MIDDLE):
            if middle_step == MIDDLE - 1:
                previous_fields = padded[:, MICRO_COUNT:-MICRO_COUNT, MICRO_COUNT:-MICRO_COUNT]
            padded = local_first(padded, depth)
            depth = depth - MICRO_COUNT
        return padded + (padded - previous_fields)

    final_fields = lax.fori_loop(
        0,
        OUTER,
        lambda present_index, state_now: forward_linear_jump(second, TOP, state_now),
        fields,
    )
    return (final_fields[0], final_fields[1])


def solution(mesh):
    return jax.shard_map(
        body,
        mesh=mesh,
        in_specs=(P("row", "col"), P("row", "col"), P("row", "col")),
        out_specs=(P("row", "col"), P("row", "col")),
        check_vma=False,
    )
```

profile of v0, /device:TPU:0, one launch (start us, length us, event | category | flops | bytes accessed | tf_op | source)
XLA Modules:
  0.0 190.3 jit_solution(8983831707697768204)
XLA Ops:
  3.2 2.5 %collective-permute-start.5 = (f32[12,1024]{1,0:T(8,128)S(1)}, f32[12,1024]{1,0:T(8,128)S(1)}, u32[]{:S(2)}, u32[]{:S(2)}) collective-permute-start(f32[12,1024]{1,0:T(8,128)S(1)} %get-tuple-element.81), channel_id=1, source_target_pairs={{16,0},{32,16},{48,32},{64,48},{80,64},{96,80},{112,96},{0,112},{1... | collective-permute-start | bytes 147464 | tf_op jit(solution)/shard_map/ppermute | solution.py:29
  5.8 2.4 %collective-permute-done.4 = f32[12,1024]{1,0:T(8,128)S(1)} collective-permute-done((f32[12,1024]{1,0:T(8,128)S(1)}, f32[12,1024]{1,0:T(8,128)S(1)}, u32[]{:S(2)}, u32[]{:S(2)}) %collective-permute-start.4) | collective-permute-done | bytes 49184 | tf_op jit(solution)/shard_map/ppermute | solution.py:26
  8.3 4.7 %collective-permute-start.7 = (f32[56,12]{1,0:T(8,128)S(1)}, f32[56,12]{1,0:T(8,128)S(1)}, u32[]{:S(2)}, u32[]{:S(2)}) collective-permute-start(f32[56,12]{1,0:T(8,128)S(1)} %get-tuple-element.78), channel_id=1, source_target_pairs={{1,0},{2,1},{3,2},{4,3},{5,4},{6,5},{7,6},{8,7},{9,8},{10,9},{11,1... | collective-permute-start | bytes 8072 | tf_op jit(solution)/shard_map/ppermute | solution.py:29
  14.6 5.3 %collective-permute-done.6 = f32[56,12]{1,0:T(8,128)S(1)} collective-permute-done((f32[56,12]{1,0:T(8,128)S(1)}, f32[56,12]{1,0:T(8,128)S(1)}, u32[]{:S(2)}, u32[]{:S(2)}) %collective-permute-start.6) | collective-permute-done | bytes 2720 | tf_op jit(solution)/shard_map/ppermute | solution.py:26
  20.1 168.5 %while.23 = (s32[]{:T(128)}, f32[2,32,1024]{2,1,0:T(8,128)}, f32[56,1048]{1,0:T(8,128)S(1)}, f32[32,1024]{1,0:T(8,128)S(1)}, s32[]{:T(128)}, /*index=5*/s32[]{:T(128)}, s32[]{:T(128)}, f32[32,1024]{1,0:T(8,128)}) while((s32[]{:T(128)}, f32[2,32,1024]{2,1,0:T(8,128)}, f32[56,1048]{1,0:T(8,128)S(1)}, f32[32,1024]{1,0:T(8,128)S(1)}, s32[]{:T(128)}, ...), condition=%wide.region_3.0_spmd, body=%wide.region_0.0_spmd.sunk | while | flops 19830928 | bytes 40506832 | solution.py:90
  21.1 83.2 %while.24 = (s32[]{:T(128)}, f32[2,32,1024]{2,1,0:T(8,128)}, f32[2,32,1024]{2,1,0:T(8,128)S(1)}, f32[56,1048]{1,0:T(8,128)S(1)}, f32[32,1024]{1,0:T(8,128)S(1)}, /*index=5*/s32[]{:T(128)}) while((s32[]{:T(128)}, f32[2,32,1024]{2,1,0:T(8,128)}, f32[2,32,1024]{2,1,0:T(8,128)S(1)}, f32[56,1048]{1,0:T(8,128)S(1)}, f32[32,1024]{1,0:T(8,128)S(1)}, ...), condition=%wide.region_2.0_spmd, body=%wide.region_1.0_spmd.sunk | while | flops 19699856 | bytes 39195972 | solution.py:57
  21.1 3.3 %collective-permute-start = (f32[2,12,1024]{2,1,0:T(8,128)S(1)}, f32[2,12,1024]{2,1,0:T(8,128)S(1)}, u32[]{:S(2)}, u32[]{:S(2)}) collective-permute-start(f32[2,12,1024]{2,1,0:T(8,128)S(1)} %get-tuple-element.157), channel_id=1, source_target_pairs={{16,0},{32,16},{48,32},{64,48},{80,64},{96,80},{112,96},{0,112},{1... | collective-permute-start | bytes 294920 | tf_op jit(solution)/shard_map/while/body/eval_jaxpr/while/body/eval_jaxpr/ppermute | solution.py:29
  24.4 2.5 %collective-permute-done = f32[2,12,1024]{2,1,0:T(8,128)S(1)} collective-permute-done((f32[2,12,1024]{2,1,0:T(8,128)S(1)}, f32[2,12,1024]{2,1,0:T(8,128)S(1)}, u32[]{:S(2)}, u32[]{:S(2)}) %collective-permute-start) | collective-permute-done | bytes 98336 | tf_op jit(solution)/shard_map/while/body/eval_jaxpr/while/body/eval_jaxpr/ppermute | solution.py:29
  26.9 4.6 %collective-permute-done.1 = f32[2,12,1024]{2,1,0:T(8,128)S(1)} collective-permute-done((f32[2,12,1024]{2,1,0:T(8,128)S(1)}, f32[2,12,1024]{2,1,0:T(8,128)S(1)}, u32[]{:S(2)}, u32[]{:S(2)}) %collective-permute-start.1) | collective-permute-done | bytes 98336 | tf_op jit(solution)/shard_map/while/body/eval_jaxpr/while/body/eval_jaxpr/ppermute | solution.py:26
  31.7 5.3 %collective-permute-start.3 = (f32[2,56,12]{2,1,0:T(8,128)S(1)}, f32[2,56,12]{2,1,0:T(8,128)S(1)}, u32[]{:S(2)}, u32[]{:S(2)}) collective-permute-start(f32[2,56,12]{2,1,0:T(8,128)S(1)} %get-tuple-element.160), channel_id=1, source_target_pairs={{1,0},{2,1},{3,2},{4,3},{5,4},{6,5},{7,6},{8,7},{9,8},{10,9},{11,1... | collective-permute-start | bytes 16136 | tf_op jit(solution)/shard_map/while/body/eval_jaxpr/while/body/eval_jaxpr/ppermute | solution.py:29
  51.0 2.0 %collective-permute-start.1 = (f32[2,12,1024]{2,1,0:T(8,128)S(1)}, f32[2,12,1024]{2,1,0:T(8,128)S(1)}, u32[]{:S(2)}, u32[]{:S(2)}) collective-permute-start(f32[2,12,1024]{2,1,0:T(8,128)S(1)} %get-tuple-element.158), channel_id=1, source_target_pairs={{0,16},{16,32},{32,48},{48,64},{64,80},{80,96},{96,112},{112,0},{1... | collective-permute-start | bytes 294920 | tf_op jit(solution)/shard_map/while/body/eval_jaxpr/while/body/eval_jaxpr/ppermute | solution.py:26
  53.0 2.9 %collective-permute-done = f32[2,12,1024]{2,1,0:T(8,128)S(1)} collective-permute-done((f32[2,12,1024]{2,1,0:T(8,128)S(1)}, f32[2,12,1024]{2,1,0:T(8,128)S(1)}, u32[]{:S(2)}, u32[]{:S(2)}) %collective-permute-start) | collective-permute-done | bytes 98336 | tf_op jit(solution)/shard_map/while/body/eval_jaxpr/while/body/eval_jaxpr/ppermute | solution.py:29
  56.0 2.2 %collective-permute-done.1 = f32[2,12,1024]{2,1,0:T(8,128)S(1)} collective-permute-done((f32[2,12,1024]{2,1,0:T(8,128)S(1)}, f32[2,12,1024]{2,1,0:T(8,128)S(1)}, u32[]{:S(2)}, u32[]{:S(2)}) %collective-permute-start.1) | collective-permute-done | bytes 98336 | tf_op jit(solution)/shard_map/while/body/eval_jaxpr/while/body/eval_jaxpr/ppermute | solution.py:26
  58.3 5.3 %collective-permute-start.3 = (f32[2,56,12]{2,1,0:T(8,128)S(1)}, f32[2,56,12]{2,1,0:T(8,128)S(1)}, u32[]{:S(2)}, u32[]{:S(2)}) collective-permute-start(f32[2,56,12]{2,1,0:T(8,128)S(1)} %get-tuple-element.160), channel_id=1, source_target_pairs={{1,0},{2,1},{3,2},{4,3},{5,4},{6,5},{7,6},{8,7},{9,8},{10,9},{11,1... | collective-permute-start | bytes 16136 | tf_op jit(solution)/shard_map/while/body/eval_jaxpr/while/body/eval_jaxpr/ppermute | solution.py:29
  77.7 2.0 %collective-permute-start.1 = (f32[2,12,1024]{2,1,0:T(8,128)S(1)}, f32[2,12,1024]{2,1,0:T(8,128)S(1)}, u32[]{:S(2)}, u32[]{:S(2)}) collective-permute-start(f32[2,12,1024]{2,1,0:T(8,128)S(1)} %get-tuple-element.158), channel_id=1, source_target_pairs={{0,16},{16,32},{32,48},{48,64},{64,80},{80,96},{96,112},{112,0},{1... | collective-permute-start | bytes 294920 | tf_op jit(solution)/shard_map/while/body/eval_jaxpr/while/body/eval_jaxpr/ppermute | solution.py:26
  79.7 2.9 %collective-permute-done = f32[2,12,1024]{2,1,0:T(8,128)S(1)} collective-permute-done((f32[2,12,1024]{2,1,0:T(8,128)S(1)}, f32[2,12,1024]{2,1,0:T(8,128)S(1)}, u32[]{:S(2)}, u32[]{:S(2)}) %collective-permute-start) | collective-permute-done | bytes 98336 | tf_op jit(solution)/shard_map/while/body/eval_jaxpr/while/body/eval_jaxpr/ppermute | solution.py:29
  82.7 2.2 %collective-permute-done.1 = f32[2,12,1024]{2,1,0:T(8,128)S(1)} collective-permute-done((f32[2,12,1024]{2,1,0:T(8,128)S(1)}, f32[2,12,1024]{2,1,0:T(8,128)S(1)}, u32[]{:S(2)}, u32[]{:S(2)}) %collective-permute-start.1) | collective-permute-done | bytes 98336 | tf_op jit(solution)/shard_map/while/body/eval_jaxpr/while/body/eval_jaxpr/ppermute | solution.py:26
  85.0 5.3 %collective-permute-start.3 = (f32[2,56,12]{2,1,0:T(8,128)S(1)}, f32[2,56,12]{2,1,0:T(8,128)S(1)}, u32[]{:S(2)}, u32[]{:S(2)}) collective-permute-start(f32[2,56,12]{2,1,0:T(8,128)S(1)} %get-tuple-element.160), channel_id=1, source_target_pairs={{1,0},{2,1},{3,2},{4,3},{5,4},{6,5},{7,6},{8,7},{9,8},{10,9},{11,1... | collective-permute-start | bytes 16136 | tf_op jit(solution)/shard_map/while/body/eval_jaxpr/while/body/eval_jaxpr/ppermute | solution.py:29
  106.9 80.0 %while.24 = (s32[]{:T(128)}, f32[2,32,1024]{2,1,0:T(8,128)}, f32[2,32,1024]{2,1,0:T(8,128)S(1)}, f32[56,1048]{1,0:T(8,128)S(1)}, f32[32,1024]{1,0:T(8,128)S(1)}, /*index=5*/s32[]{:T(128)}) while((s32[]{:T(128)}, f32[2,32,1024]{2,1,0:T(8,128)}, f32[2,32,1024]{2,1,0:T(8,128)S(1)}, f32[56,1048]{1,0:T(8,128)S(1)}, f32[32,1024]{1,0:T(8,128)S(1)}, ...), condition=%wide.region_2.0_spmd, body=%wide.region_1.0_spmd.sunk | while | flops 19699856 | bytes 39195972 | solution.py:57
  107.0 2.0 %collective-permute-start.1 = (f32[2,12,1024]{2,1,0:T(8,128)S(1)}, f32[2,12,1024]{2,1,0:T(8,128)S(1)}, u32[]{:S(2)}, u32[]{:S(2)}) collective-permute-start(f32[2,12,1024]{2,1,0:T(8,128)S(1)} %get-tuple-element.158), channel_id=1, source_target_pairs={{0,16},{16,32},{32,48},{48,64},{64,80},{80,96},{96,112},{112,0},{1... | collective-permute-start | bytes 294920 | tf_op jit(solution)/shard_map/while/body/eval_jaxpr/while/body/eval_jaxpr/ppermute | solution.py:26
  109.0 2.9 %collective-permute-done = f32[2,12,1024]{2,1,0:T(8,128)S(1)} collective-permute-done((f32[2,12,1024]{2,1,0:T(8,128)S(1)}, f32[2,12,1024]{2,1,0:T(8,128)S(1)}, u32[]{:S(2)}, u32[]{:S(2)}) %collective-permute-start) | collective-permute-done | bytes 98336 | tf_op jit(solution)/shard_map/while/body/eval_jaxpr/while/body/eval_jaxpr/ppermute | solution.py:29
  112.0 2.2 %collective-permute-done.1 = f32[2,12,1024]{2,1,0:T(8,128)S(1)} collective-permute-done((f32[2,12,1024]{2,1,0:T(8,128)S(1)}, f32[2,12,1024]{2,1,0:T(8,128)S(1)}, u32[]{:S(2)}, u32[]{:S(2)}) %collective-permute-start.1) | collective-permute-done | bytes 98336 | tf_op jit(solution)/shard_map/while/body/eval_jaxpr/while/body/eval_jaxpr/ppermute | solution.py:26
  114.3 5.3 %collective-permute-start.3 = (f32[2,56,12]{2,1,0:T(8,128)S(1)}, f32[2,56,12]{2,1,0:T(8,128)S(1)}, u32[]{:S(2)}, u32[]{:S(2)}) collective-permute-start(f32[2,56,12]{2,1,0:T(8,128)S(1)} %get-tuple-element.160), channel_id=1, source_target_pairs={{1,0},{2,1},{3,2},{4,3},{5,4},{6,5},{7,6},{8,7},{9,8},{10,9},{11,1... | collective-permute-start | bytes 16136 | tf_op jit(solution)/shard_map/while/body/eval_jaxpr/while/body/eval_jaxpr/ppermute | solution.py:29
  133.7 2.0 %collective-permute-start.1 = (f32[2,12,1024]{2,1,0:T(8,128)S(1)}, f32[2,12,1024]{2,1,0:T(8,128)S(1)}, u32[]{:S(2)}, u32[]{:S(2)}) collective-permute-start(f32[2,12,1024]{2,1,0:T(8,128)S(1)} %get-tuple-element.158), channel_id=1, source_target_pairs={{0,16},{16,32},{32,48},{48,64},{64,80},{80,96},{96,112},{112,0},{1... | collective-permute-start | bytes 294920 | tf_op jit(solution)/shard_map/while/body/eval_jaxpr/while/body/eval_jaxpr/ppermute | solution.py:26
  135.7 2.9 %collective-permute-done = f32[2,12,1024]{2,1,0:T(8,128)S(1)} collective-permute-done((f32[2,12,1024]{2,1,0:T(8,128)S(1)}, f32[2,12,1024]{2,1,0:T(8,128)S(1)}, u32[]{:S(2)}, u32[]{:S(2)}) %collective-permute-start) | collective-permute-done | bytes 98336 | tf_op jit(solution)/shard_map/while/body/eval_jaxpr/while/body/eval_jaxpr/ppermute | solution.py:29
  138.6 2.2 %collective-permute-done.1 = f32[2,12,1024]{2,1,0:T(8,128)S(1)} collective-permute-done((f32[2,12,1024]{2,1,0:T(8,128)S(1)}, f32[2,12,1024]{2,1,0:T(8,128)S(1)}, u32[]{:S(2)}, u32[]{:S(2)}) %collective-permute-start.1) | collective-permute-done | bytes 98336 | tf_op jit(solution)/shard_map/while/body/eval_jaxpr/while/body/eval_jaxpr/ppermute | solution.py:26
  141.0 5.3 %collective-permute-start.3 = (f32[2,56,12]{2,1,0:T(8,128)S(1)}, f32[2,56,12]{2,1,0:T(8,128)S(1)}, u32[]{:S(2)}, u32[]{:S(2)}) collective-permute-start(f32[2,56,12]{2,1,0:T(8,128)S(1)} %get-tuple-element.160), channel_id=1, source_target_pairs={{1,0},{2,1},{3,2},{4,3},{5,4},{6,5},{7,6},{8,7},{9,8},{10,9},{11,1... | collective-permute-start | bytes 16136 | tf_op jit(solution)/shard_map/while/body/eval_jaxpr/while/body/eval_jaxpr/ppermute | solution.py:29
  160.4 2.0 %collective-permute-start.1 = (f32[2,12,1024]{2,1,0:T(8,128)S(1)}, f32[2,12,1024]{2,1,0:T(8,128)S(1)}, u32[]{:S(2)}, u32[]{:S(2)}) collective-permute-start(f32[2,12,1024]{2,1,0:T(8,128)S(1)} %get-tuple-element.158), channel_id=1, source_target_pairs={{0,16},{16,32},{32,48},{48,64},{64,80},{80,96},{96,112},{112,0},{1... | collective-permute-start | bytes 294920 | tf_op jit(solution)/shard_map/while/body/eval_jaxpr/while/body/eval_jaxpr/ppermute | solution.py:26
  162.4 2.9 %collective-permute-done = f32[2,12,1024]{2,1,0:T(8,128)S(1)} collective-permute-done((f32[2,12,1024]{2,1,0:T(8,128)S(1)}, f32[2,12,1024]{2,1,0:T(8,128)S(1)}, u32[]{:S(2)}, u32[]{:S(2)}) %collective-permute-start) | collective-permute-done | bytes 98336 | tf_op jit(solution)/shard_map/while/body/eval_jaxpr/while/body/eval_jaxpr/ppermute | solution.py:29
  165.3 2.2 %collective-permute-done.1 = f32[2,12,1024]{2,1,0:T(8,128)S(1)} collective-permute-done((f32[2,12,1024]{2,1,0:T(8,128)S(1)}, f32[2,12,1024]{2,1,0:T(8,128)S(1)}, u32[]{:S(2)}, u32[]{:S(2)}) %collective-permute-start.1) | collective-permute-done | bytes 98336 | tf_op jit(solution)/shard_map/while/body/eval_jaxpr/while/body/eval_jaxpr/ppermute | solution.py:26
  167.7 5.3 %collective-permute-start.3 = (f32[2,56,12]{2,1,0:T(8,128)S(1)}, f32[2,56,12]{2,1,0:T(8,128)S(1)}, u32[]{:S(2)}, u32[]{:S(2)}) collective-permute-start(f32[2,56,12]{2,1,0:T(8,128)S(1)} %get-tuple-element.160), channel_id=1, source_target_pairs={{1,0},{2,1},{3,2},{4,3},{5,4},{6,5},{7,6},{8,7},{9,8},{10,9},{11,1... | collective-permute-start | bytes 16136 | tf_op jit(solution)/shard_map/while/body/eval_jaxpr/while/body/eval_jaxpr/ppermute | solution.py:29
  188.6 1.7 slice_bitcast_fusion
  (303 shorter events, 93.1 us)
Async XLA Ops:
  0.6 7.6 %copy-start = (f32[32,1024]{1,0:T(8,128)S(1)}, f32[32,1024]{1,0:T(8,128)}, u32[]{:S(2)}) copy-start(f32[32,1024]{1,0:T(8,128)} %param.9) | copy-start | bytes 393220
  1.6 6.6 %collective-permute-start.4 = (f32[12,1024]{1,0:T(8,128)S(1)}, f32[12,1024]{1,0:T(8,128)S(1)}, u32[]{:S(2)}, u32[]{:S(2)}) collective-permute-start(f32[12,1024]{1,0:T(8,128)S(1)} %get-tuple-element.80), channel_id=1, source_target_pairs={{0,16},{16,32},{32,48},{48,64},{64,80},{80,96},{96,112},{112,0},{1... | collective-permute-start | bytes 147464 | tf_op jit(solution)/shard_map/ppermute | solution.py:26
  3.2 4.9 %collective-permute-start.5 = (f32[12,1024]{1,0:T(8,128)S(1)}, f32[12,1024]{1,0:T(8,128)S(1)}, u32[]{:S(2)}, u32[]{:S(2)}) collective-permute-start(f32[12,1024]{1,0:T(8,128)S(1)} %get-tuple-element.81), channel_id=1, source_target_pairs={{16,0},{32,16},{48,32},{64,48},{80,64},{96,80},{112,96},{0,112},{1... | collective-permute-start | bytes 147464 | tf_op jit(solution)/shard_map/ppermute | solution.py:29
  8.2 4.9 %copy-start.2 = (f32[32,1024]{1,0:T(8,128)S(1)}, f32[32,1024]{1,0:T(8,128)}, u32[]{:S(2)}) copy-start(f32[32,1024]{1,0:T(8,128)} %param.8) | copy-start | bytes 393220
  8.2 4.9 %copy-start.3 = (f32[32,1024]{1,0:T(8,128)S(1)}, f32[32,1024]{1,0:T(8,128)}, u32[]{:S(2)}) copy-start(f32[32,1024]{1,0:T(8,128)} %param.7) | copy-start | bytes 393220
  8.3 6.3 %collective-permute-start.7 = (f32[56,12]{1,0:T(8,128)S(1)}, f32[56,12]{1,0:T(8,128)S(1)}, u32[]{:S(2)}, u32[]{:S(2)}) collective-permute-start(f32[56,12]{1,0:T(8,128)S(1)} %get-tuple-element.78), channel_id=1, source_target_pairs={{1,0},{2,1},{3,2},{4,3},{5,4},{6,5},{7,6},{8,7},{9,8},{10,9},{11,1... | collective-permute-start | bytes 8072 | tf_op jit(solution)/shard_map/ppermute | solution.py:29
  13.1 6.9 %collective-permute-start.6 = (f32[56,12]{1,0:T(8,128)S(1)}, f32[56,12]{1,0:T(8,128)S(1)}, u32[]{:S(2)}, u32[]{:S(2)}) collective-permute-start(f32[56,12]{1,0:T(8,128)S(1)} %get-tuple-element.79), channel_id=1, source_target_pairs={{0,1},{1,2},{2,3},{3,4},{4,5},{5,6},{6,7},{7,8},{8,9},{9,10},{10,1... | collective-permute-start | bytes 8072 | tf_op jit(solution)/shard_map/ppermute | solution.py:26
  13.8 6.4 %copy-start.1 = (f32[32,1024]{1,0:T(8,128)S(1)}, f32[32,1024]{1,0:T(8,128)}, u32[]{:S(2)}) copy-start(f32[32,1024]{1,0:T(8,128)} %param.9) | copy-start | bytes 393220
  21.1 5.8 %collective-permute-start = (f32[2,12,1024]{2,1,0:T(8,128)S(1)}, f32[2,12,1024]{2,1,0:T(8,128)S(1)}, u32[]{:S(2)}, u32[]{:S(2)}) collective-permute-start(f32[2,12,1024]{2,1,0:T(8,128)S(1)} %get-tuple-element.157), channel_id=1, source_target_pairs={{16,0},{32,16},{48,32},{64,48},{80,64},{96,80},{112,96},{0,112},{1... | collective-permute-start | bytes 294920 | tf_op jit(solution)/shard_map/while/body/eval_jaxpr/while/body/eval_jaxpr/ppermute | solution.py:29
  24.4 7.1 %collective-permute-start.1 = (f32[2,12,1024]{2,1,0:T(8,128)S(1)}, f32[2,12,1024]{2,1,0:T(8,128)S(1)}, u32[]{:S(2)}, u32[]{:S(2)}) collective-permute-start(f32[2,12,1024]{2,1,0:T(8,128)S(1)} %get-tuple-element.158), channel_id=1, source_target_pairs={{0,16},{16,32},{32,48},{48,64},{64,80},{80,96},{96,112},{112,0},{1... | collective-permute-start | bytes 294920 | tf_op jit(solution)/shard_map/while/body/eval_jaxpr/while/body/eval_jaxpr/ppermute | solution.py:26
  31.6 7.2 %collective-permute-start.2 = (f32[2,56,12]{2,1,0:T(8,128)S(1)}, f32[2,56,12]{2,1,0:T(8,128)S(1)}, u32[]{:S(2)}, u32[]{:S(2)}) collective-permute-start(f32[2,56,12]{2,1,0:T(8,128)S(1)} %get-tuple-element.159), channel_id=1, source_target_pairs={{0,1},{1,2},{2,3},{3,4},{4,5},{5,6},{6,7},{7,8},{8,9},{9,10},{10,1... | collective-permute-start | bytes 16136 | tf_op jit(solution)/shard_map/while/body/eval_jaxpr/while/body/eval_jaxpr/ppermute | solution.py:26
  31.7 7.2 %collective-permute-start.3 = (f32[2,56,12]{2,1,0:T(8,128)S(1)}, f32[2,56,12]{2,1,0:T(8,128)S(1)}, u32[]{:S(2)}, u32[]{:S(2)}) collective-permute-start(f32[2,56,12]{2,1,0:T(8,128)S(1)} %get-tuple-element.160), channel_id=1, source_target_pairs={{1,0},{2,1},{3,2},{4,3},{5,4},{6,5},{7,6},{8,7},{9,8},{10,9},{11,1... | collective-permute-start | bytes 16136 | tf_op jit(solution)/shard_map/while/body/eval_jaxpr/while/body/eval_jaxpr/ppermute | solution.py:29
  51.0 5.0 %collective-permute-start = (f32[2,12,1024]{2,1,0:T(8,128)S(1)}, f32[2,12,1024]{2,1,0:T(8,128)S(1)}, u32[]{:S(2)}, u32[]{:S(2)}) collective-permute-start(f32[2,12,1024]{2,1,0:T(8,128)S(1)} %get-tuple-element.157), channel_id=1, source_target_pairs={{16,0},{32,16},{48,32},{64,48},{80,64},{96,80},{112,96},{0,112},{1... | collective-permute-start | bytes 294920 | tf_op jit(solution)/shard_map/while/body/eval_jaxpr/while/body/eval_jaxpr/ppermute | solution.py:29
  51.0 7.1 %collective-permute-start.1 = (f32[2,12,1024]{2,1,0:T(8,128)S(1)}, f32[2,12,1024]{2,1,0:T(8,128)S(1)}, u32[]{:S(2)}, u32[]{:S(2)}) collective-permute-start(f32[2,12,1024]{2,1,0:T(8,128)S(1)} %get-tuple-element.158), channel_id=1, source_target_pairs={{0,16},{16,32},{32,48},{48,64},{64,80},{80,96},{96,112},{112,0},{1... | collective-permute-start | bytes 294920 | tf_op jit(solution)/shard_map/while/body/eval_jaxpr/while/body/eval_jaxpr/ppermute | solution.py:26
  58.3 7.2 %collective-permute-start.2 = (f32[2,56,12]{2,1,0:T(8,128)S(1)}, f32[2,56,12]{2,1,0:T(8,128)S(1)}, u32[]{:S(2)}, u32[]{:S(2)}) collective-permute-start(f32[2,56,12]{2,1,0:T(8,128)S(1)} %get-tuple-element.159), channel_id=1, source_target_pairs={{0,1},{1,2},{2,3},{3,4},{4,5},{5,6},{6,7},{7,8},{8,9},{9,10},{10,1... | collective-permute-start | bytes 16136 | tf_op jit(solution)/shard_map/while/body/eval_jaxpr/while/body/eval_jaxpr/ppermute | solution.py:26
  58.3 7.2 %collective-permute-start.3 = (f32[2,56,12]{2,1,0:T(8,128)S(1)}, f32[2,56,12]{2,1,0:T(8,128)S(1)}, u32[]{:S(2)}, u32[]{:S(2)}) collective-permute-start(f32[2,56,12]{2,1,0:T(8,128)S(1)} %get-tuple-element.160), channel_id=1, source_target_pairs={{1,0},{2,1},{3,2},{4,3},{5,4},{6,5},{7,6},{8,7},{9,8},{10,9},{11,1... | collective-permute-start | bytes 16136 | tf_op jit(solution)/shard_map/while/body/eval_jaxpr/while/body/eval_jaxpr/ppermute | solution.py:29
  77.6 5.0 %collective-permute-start = (f32[2,12,1024]{2,1,0:T(8,128)S(1)}, f32[2,12,1024]{2,1,0:T(8,128)S(1)}, u32[]{:S(2)}, u32[]{:S(2)}) collective-permute-start(f32[2,12,1024]{2,1,0:T(8,128)S(1)} %get-tuple-element.157), channel_id=1, source_target_pairs={{16,0},{32,16},{48,32},{64,48},{80,64},{96,80},{112,96},{0,112},{1... | collective-permute-start | bytes 294920 | tf_op jit(solution)/shard_map/while/body/eval_jaxpr/while/body/eval_jaxpr/ppermute | solution.py:29
  77.7 7.1 %collective-permute-start.1 = (f32[2,12,1024]{2,1,0:T(8,128)S(1)}, f32[2,12,1024]{2,1,0:T(8,128)S(1)}, u32[]{:S(2)}, u32[]{:S(2)}) collective-permute-start(f32[2,12,1024]{2,1,0:T(8,128)S(1)} %get-tuple-element.158), channel_id=1, source_target_pairs={{0,16},{16,32},{32,48},{48,64},{64,80},{80,96},{96,112},{112,0},{1... | collective-permute-start | bytes 294920 | tf_op jit(solution)/shard_map/while/body/eval_jaxpr/while/body/eval_jaxpr/ppermute | solution.py:26
  85.0 7.2 %collective-permute-start.2 = (f32[2,56,12]{2,1,0:T(8,128)S(1)}, f32[2,56,12]{2,1,0:T(8,128)S(1)}, u32[]{:S(2)}, u32[]{:S(2)}) collective-permute-start(f32[2,56,12]{2,1,0:T(8,128)S(1)} %get-tuple-element.159), channel_id=1, source_target_pairs={{0,1},{1,2},{2,3},{3,4},{4,5},{5,6},{6,7},{7,8},{8,9},{9,10},{10,1... | collective-permute-start | bytes 16136 | tf_op jit(solution)/shard_map/while/body/eval_jaxpr/while/body/eval_jaxpr/ppermute | solution.py:26
  85.0 7.2 %collective-permute-start.3 = (f32[2,56,12]{2,1,0:T(8,128)S(1)}, f32[2,56,12]{2,1,0:T(8,128)S(1)}, u32[]{:S(2)}, u32[]{:S(2)}) collective-permute-start(f32[2,56,12]{2,1,0:T(8,128)S(1)} %get-tuple-element.160), channel_id=1, source_target_pairs={{1,0},{2,1},{3,2},{4,3},{5,4},{6,5},{7,6},{8,7},{9,8},{10,9},{11,1... | collective-permute-start | bytes 16136 | tf_op jit(solution)/shard_map/while/body/eval_jaxpr/while/body/eval_jaxpr/ppermute | solution.py:29
  106.9 5.0 %collective-permute-start = (f32[2,12,1024]{2,1,0:T(8,128)S(1)}, f32[2,12,1024]{2,1,0:T(8,128)S(1)}, u32[]{:S(2)}, u32[]{:S(2)}) collective-permute-start(f32[2,12,1024]{2,1,0:T(8,128)S(1)} %get-tuple-element.157), channel_id=1, source_target_pairs={{16,0},{32,16},{48,32},{64,48},{80,64},{96,80},{112,96},{0,112},{1... | collective-permute-start | bytes 294920 | tf_op jit(solution)/shard_map/while/body/eval_jaxpr/while/body/eval_jaxpr/ppermute | solution.py:29
  107.0 7.1 %collective-permute-start.1 = (f32[2,12,1024]{2,1,0:T(8,128)S(1)}, f32[2,12,1024]{2,1,0:T(8,128)S(1)}, u32[]{:S(2)}, u32[]{:S(2)}) collective-permute-start(f32[2,12,1024]{2,1,0:T(8,128)S(1)} %get-tuple-element.158), channel_id=1, source_target_pairs={{0,16},{16,32},{32,48},{48,64},{64,80},{80,96},{96,112},{112,0},{1... | collective-permute-start | bytes 294920 | tf_op jit(solution)/shard_map/while/body/eval_jaxpr/while/body/eval_jaxpr/ppermute | solution.py:26
  114.3 7.2 %collective-permute-start.2 = (f32[2,56,12]{2,1,0:T(8,128)S(1)}, f32[2,56,12]{2,1,0:T(8,128)S(1)}, u32[]{:S(2)}, u32[]{:S(2)}) collective-permute-start(f32[2,56,12]{2,1,0:T(8,128)S(1)} %get-tuple-element.159), channel_id=1, source_target_pairs={{0,1},{1,2},{2,3},{3,4},{4,5},{5,6},{6,7},{7,8},{8,9},{9,10},{10,1... | collective-permute-start | bytes 16136 | tf_op jit(solution)/shard_map/while/body/eval_jaxpr/while/body/eval_jaxpr/ppermute | solution.py:26
  114.3 7.2 %collective-permute-start.3 = (f32[2,56,12]{2,1,0:T(8,128)S(1)}, f32[2,56,12]{2,1,0:T(8,128)S(1)}, u32[]{:S(2)}, u32[]{:S(2)}) collective-permute-start(f32[2,56,12]{2,1,0:T(8,128)S(1)} %get-tuple-element.160), channel_id=1, source_target_pairs={{1,0},{2,1},{3,2},{4,3},{5,4},{6,5},{7,6},{8,7},{9,8},{10,9},{11,1... | collective-permute-start | bytes 16136 | tf_op jit(solution)/shard_map/while/body/eval_jaxpr/while/body/eval_jaxpr/ppermute | solution.py:29
  133.6 5.0 %collective-permute-start = (f32[2,12,1024]{2,1,0:T(8,128)S(1)}, f32[2,12,1024]{2,1,0:T(8,128)S(1)}, u32[]{:S(2)}, u32[]{:S(2)}) collective-permute-start(f32[2,12,1024]{2,1,0:T(8,128)S(1)} %get-tuple-element.157), channel_id=1, source_target_pairs={{16,0},{32,16},{48,32},{64,48},{80,64},{96,80},{112,96},{0,112},{1... | collective-permute-start | bytes 294920 | tf_op jit(solution)/shard_map/while/body/eval_jaxpr/while/body/eval_jaxpr/ppermute | solution.py:29
  133.7 7.1 %collective-permute-start.1 = (f32[2,12,1024]{2,1,0:T(8,128)S(1)}, f32[2,12,1024]{2,1,0:T(8,128)S(1)}, u32[]{:S(2)}, u32[]{:S(2)}) collective-permute-start(f32[2,12,1024]{2,1,0:T(8,128)S(1)} %get-tuple-element.158), channel_id=1, source_target_pairs={{0,16},{16,32},{32,48},{48,64},{64,80},{80,96},{96,112},{112,0},{1... | collective-permute-start | bytes 294920 | tf_op jit(solution)/shard_map/while/body/eval_jaxpr/while/body/eval_jaxpr/ppermute | solution.py:26
  141.0 7.2 %collective-permute-start.2 = (f32[2,56,12]{2,1,0:T(8,128)S(1)}, f32[2,56,12]{2,1,0:T(8,128)S(1)}, u32[]{:S(2)}, u32[]{:S(2)}) collective-permute-start(f32[2,56,12]{2,1,0:T(8,128)S(1)} %get-tuple-element.159), channel_id=1, source_target_pairs={{0,1},{1,2},{2,3},{3,4},{4,5},{5,6},{6,7},{7,8},{8,9},{9,10},{10,1... | collective-permute-start | bytes 16136 | tf_op jit(solution)/shard_map/while/body/eval_jaxpr/while/body/eval_jaxpr/ppermute | solution.py:26
  141.0 7.2 %collective-permute-start.3 = (f32[2,56,12]{2,1,0:T(8,128)S(1)}, f32[2,56,12]{2,1,0:T(8,128)S(1)}, u32[]{:S(2)}, u32[]{:S(2)}) collective-permute-start(f32[2,56,12]{2,1,0:T(8,128)S(1)} %get-tuple-element.160), channel_id=1, source_target_pairs={{1,0},{2,1},{3,2},{4,3},{5,4},{6,5},{7,6},{8,7},{9,8},{10,9},{11,1... | collective-permute-start | bytes 16136 | tf_op jit(solution)/shard_map/while/body/eval_jaxpr/while/body/eval_jaxpr/ppermute | solution.py:29
  160.3 5.0 %collective-permute-start = (f32[2,12,1024]{2,1,0:T(8,128)S(1)}, f32[2,12,1024]{2,1,0:T(8,128)S(1)}, u32[]{:S(2)}, u32[]{:S(2)}) collective-permute-start(f32[2,12,1024]{2,1,0:T(8,128)S(1)} %get-tuple-element.157), channel_id=1, source_target_pairs={{16,0},{32,16},{48,32},{64,48},{80,64},{96,80},{112,96},{0,112},{1... | collective-permute-start | bytes 294920 | tf_op jit(solution)/shard_map/while/body/eval_jaxpr/while/body/eval_jaxpr/ppermute | solution.py:29
  160.4 7.1 %collective-permute-start.1 = (f32[2,12,1024]{2,1,0:T(8,128)S(1)}, f32[2,12,1024]{2,1,0:T(8,128)S(1)}, u32[]{:S(2)}, u32[]{:S(2)}) collective-permute-start(f32[2,12,1024]{2,1,0:T(8,128)S(1)} %get-tuple-element.158), channel_id=1, source_target_pairs={{0,16},{16,32},{32,48},{48,64},{64,80},{80,96},{96,112},{112,0},{1... | collective-permute-start | bytes 294920 | tf_op jit(solution)/shard_map/while/body/eval_jaxpr/while/body/eval_jaxpr/ppermute | solution.py:26
  167.6 7.2 %collective-permute-start.2 = (f32[2,56,12]{2,1,0:T(8,128)S(1)}, f32[2,56,12]{2,1,0:T(8,128)S(1)}, u32[]{:S(2)}, u32[]{:S(2)}) collective-permute-start(f32[2,56,12]{2,1,0:T(8,128)S(1)} %get-tuple-element.159), channel_id=1, source_target_pairs={{0,1},{1,2},{2,3},{3,4},{4,5},{5,6},{6,7},{7,8},{8,9},{9,10},{10,1... | collective-permute-start | bytes 16136 | tf_op jit(solution)/shard_map/while/body/eval_jaxpr/while/body/eval_jaxpr/ppermute | solution.py:26
  167.7 7.2 %collective-permute-start.3 = (f32[2,56,12]{2,1,0:T(8,128)S(1)}, f32[2,56,12]{2,1,0:T(8,128)S(1)}, u32[]{:S(2)}, u32[]{:S(2)}) collective-permute-start(f32[2,56,12]{2,1,0:T(8,128)S(1)} %get-tuple-element.160), channel_id=1, source_target_pairs={{1,0},{2,1},{3,2},{4,3},{5,4},{6,5},{7,6},{8,7},{9,8},{10,9},{11,1... | collective-permute-start | bytes 16136 | tf_op jit(solution)/shard_map/while/body/eval_jaxpr/while/body/eval_jaxpr/ppermute | solution.py:29
where the time goes:
time: 191 us; the launch traced here: 190 us
  other arithmetic  73.5 us (38%)
  starting transfers between devices  54.9 us (29%)
  waiting for transfers between devices  48.3 us (25%)
  local copies, waits for them, and re-layouts  11.3 us (6%)
    ppermute x14, starting transfers between devices, extended(): lax.ppermute(lax.slice_in_dim(block, 0, width, axis=dim), axis, backward)  43 us
    sub x72, other arithmetic, advance(): beside_all = beside_all - 4.0 * centre  36.3 us
    ppermute x14, waiting for transfers between devices, extended(): lax.ppermute(lax.slice_in_dim(block, block.shape[dim] - width, None, axis...  30.3 us
    ppermute x14, waiting for transfers between devices, extended(): lax.ppermute(lax.slice_in_dim(block, 0, width, axis=dim), axis, backward)  18.1 us
    another operation x66, other arithmetic, advance(): return jnp.stack([u_next, v_next])  16.2 us
    add x66, other arithmetic, advance(): v_now + RATE_V * beside_all[1]  12.3 us
    ppermute x14, starting transfers between devices, extended(): lax.ppermute(lax.slice_in_dim(block, block.shape[dim] - width, None, axis...  11.9 us
    while x8, local copies, waits for them, and re-layouts  6.04 us
  transfers between devices with their start and end apart: 28, of which 21 were waited for; matrix products, arithmetic and copies ran while one was open for 3% of the time, Pallas kernels for 0%

commit v1 on v0

v1 whole, which is shorter than its diff:
```python
import jax
import jax.numpy as jnp
from jax import lax
from jax.experimental import pallas as pl
from jax.experimental.pallas import tpu as pltpu
from jax.sharding import PartitionSpec as P

MESH = pl.DeviceIdType.MESH

MICRO_COUNT = 4
MIDDLE = 3
TOP = 3
OUTER = 2

SCALE = 7.5**0.5
SHIFT = 0.875
KEEP_U = 4.4
KEEP_V = 3.9744
COUPLE = 0.0128

STRIP = 128
HALO = 40
STEPS = TOP * MIDDLE * MICRO_COUNT
WIDE = STRIP + 2 * HALO


def place(chip, core):
    group, spot = lax.div(chip, 8), lax.rem(chip, 8)
    half = lax.div(spot, 4)
    y = half * (7 - spot) + (1 - half) * spot
    x = lax.rem(half + lax.div(group, 4) + lax.rem(group, 4), 2)
    return (2 * y + x, 2 * group + core)


def fine(src, stim, dst, low, count, kind, previous=None, before=None):
    u0 = src[0, low : low + count, :]
    u1 = src[1, low : low + count, :]
    v0 = src[2, low : low + count, :]
    v1 = src[3, low : low + count, :]

    def column(i):
        return src[i, low - 1 : low - 1 + count, :] + src[i, low + 1 : low + 1 + count, :]

    keep_u, keep_v, rate = KEEP_U, KEEP_V, 0.125
    if kind > 0:
        keep_u, keep_v, rate = KEEP_U - 4.0, KEEP_V - 4.0, 0.125 * 2**kind
    su0 = column(0) + (u1 + pltpu.roll(u1, 1, 1))
    su1 = column(1) + (u0 + pltpu.roll(u0, 127, 1))
    sv0 = column(2) + (v1 + pltpu.roll(v1, 1, 1))
    sv1 = column(3) + (v0 + pltpu.roll(v0, 127, 1))
    s0 = stim[4, low : low + count, :]
    s1 = stim[5, low : low + count, :]
    new = [
        (su0 + u0 * (keep_u - u0 * u0)) + (s0 - v0),
        (su1 + u1 * (keep_u - u1 * u1)) + (s1 - v1),
        sv0 + (keep_v * v0 + COUPLE * u0),
        sv1 + (keep_v * v1 + COUPLE * u1),
    ]
    for i in range(4):
        value = new[i] if rate == 1.0 else rate * new[i]
        if kind == 2:
            value = value - previous[i, low : low + count, :]
        if kind == 3:
            twice = previous[i, low : low + count, :]
            value = value - (twice + twice) - before[i, low : low + count, :]
        dst[i, low : low + count, :] = value


def kernel(
    u_in, v_in, s_in, u_out, v_out,
    loaded, rows, first, second, ping, pong, t_one, t_two, y_one, y_two, last, result,
    load_sem, in_send, in_recv, halo_send, halo_recv, out_send, out_recv,
):
    row, col = lax.axis_index("row"), lax.axis_index("col")
    y, x = lax.div(row, 2), lax.rem(row, 2)
    group, core = lax.div(col, 2), lax.rem(col, 2)
    turned = lax.rem(lax.div(group, 4) + lax.rem(group, 4), 2)
    half = lax.rem(x + turned, 2)
    spot = half * (7 - y) + (1 - half) * y
    chip = 8 * group + spot
    own = half * (6 - 2 * y) + (1 - half) * 2 * y + core
    here = half == core
    across = lax.rem(core + turned, 2)

    inputs = (u_in, v_in, s_in)
    loads = [
        pltpu.make_async_copy(inputs[i], loaded.at[i], load_sem.at[i]) for i in range(3)
    ]
    for load in loads:
        load.start()

    left = place(lax.rem(chip + 63 + core, 64), 1 - core)
    right = place(lax.rem(chip + core, 64), 1 - core)

    def target(i):
        to_y = lax.rem(y + (2, 1, 3, 0)[i // 2], 4)
        to_core = lax.rem(core + 1 + i, 2)
        tile = core * (6 - 2 * to_y) + (1 - core) * 2 * to_y + to_core
        return (2 * to_y + across, 2 * group + to_core), tile

    def source(i):
        return lax.rem(row + i, 8)

    barrier = pltpu.get_barrier_semaphore()

    def greet(device):
        pl.semaphore_signal(barrier, inc=1, device_id=device, device_id_type=MESH)

    for i in range(7):
        greet(target(i)[0])
        greet((source(i + 1), 2 * group + half))

    @pl.when(jnp.logical_not(here))
    def _():
        greet(target(7)[0])
        greet((source(0), 2 * group + half))

    greet(left)
    greet(right)
    pl.semaphore_wait(barrier, 16 + 2 * (1 - jnp.where(here, 1, 0)))

    def lanes(tile):
        return pl.ds(pl.multiple_of(tile * 128, 128), 128)

    def piece(where):
        return pl.ds(pl.multiple_of(where * 32, 32), 32)

    def moved_in(field, i):
        device, tile = target(i)
        return pltpu.make_async_remote_copy(
            src_ref=loaded.at[field, :, lanes(tile)],
            dst_ref=rows.at[field, piece(row)],
            send_sem=in_send.at[field, i],
            recv_sem=in_recv.at[field, row],
            device_id=device,
            device_id_type=MESH,
        )

    def kept_in(field):
        return pltpu.make_async_copy(
            inputs[field].at[:, lanes(own)], rows.at[field, piece(row)], in_recv.at[field, row]
        )

    for field in range(3):
        loads[field].wait()
        for i in range(7):
            moved_in(field, i).start()

        @pl.when(here)
        def _():
            kept_in(field).start()

        @pl.when(jnp.logical_not(here))
        def _():
            moved_in(field, 7).start()

    def edge(buffer, planes, which, side):
        mine, theirs = ((HALO, WIDE - HALO), (WIDE - 2 * HALO, 0))[side]
        return pltpu.make_async_remote_copy(
            src_ref=buffer.at[planes, pl.ds(mine, HALO)],
            dst_ref=buffer.at[planes, pl.ds(theirs, HALO)],
            send_sem=halo_send.at[which, side],
            recv_sem=halo_recv.at[which, side],
            device_id=(left, right)[side],
            device_id_type=MESH,
        )

    edges = []
    for field in range(3):
        for sender in range(8):
            pltpu.make_async_copy(
                inputs[field].at[:, pl.ds(0, 128)],
                rows.at[field, pl.ds(32 * sender, 32)],
                in_recv.at[field, sender],
            ).wait()
        for parity in range(2):
            block = rows[field, pl.ds(parity, 128, stride=2), :].T
            if field == 0:
                block = block * (1.0 / SCALE)
            else:
                block = (block - SHIFT) * (0.4 / SCALE)
            first[2 * field + parity, HALO : HALO + STRIP, :] = block
        for side in range(2):
            copy = edge(first, pl.ds(2 * field, 2), field, side)
            copy.start()
            edges.append(copy)
    for copy in edges:
        copy.wait()

    start = first
    for outer in range(OUTER):
        done = 0
        state = start
        goal = (second, last)[outer]
        for top in range(TOP):
            for middle in range(MIDDLE):
                end = (t_one, t_two, (y_one, y_two, goal)[top])[middle]
                for micro in range(MICRO_COUNT):
                    done += 1
                    low = HALO - STEPS + done
                    count = -(-(WIDE - 2 * low) // 8) * 8
                    ends = micro == MICRO_COUNT - 1
                    kind = 0
                    if ends:
                        kind = 1 + (middle == MIDDLE - 1) * (1 + (top == TOP - 1))
                    into = end if ends else (ping, pong)[micro % 2]
                    fine(state, first, into, low, count, kind, t_two, y_two)
                    state = into
        start = goal
        if outer < OUTER - 1:
            edges = [edge(second, pl.ds(0, 4), 3 + outer, side) for side in range(2)]
            for copy in edges:
                copy.start()
            for copy in edges:
                copy.wait()

    outputs = (u_out, v_out)

    def moved_out(field, i):
        to = source(i)
        return pltpu.make_async_remote_copy(
            src_ref=result.at[field, piece(to)],
            dst_ref=outputs[field].at[:, lanes(own)],
            send_sem=out_send.at[field, i],
            recv_sem=out_recv.at[field, own],
            device_id=(to, 2 * group + half),
            device_id_type=MESH,
        )

    for field in range(2):
        for parity in range(2):
            block = last[2 * field + parity, HALO : HALO + STRIP, :]
            if field == 0:
                block = block * SCALE
            else:
                block = block * (SCALE / 0.4) + SHIFT
            result[field, pl.ds(parity, 128, stride=2), :] = block.T
        for i in range(1, 8):
            moved_out(field, i).start()

        @pl.when(jnp.logical_not(here))
        def _():
            moved_out(field, 0).start()

        @pl.when(here)
        def _():
            outputs[field][:, lanes(own)] = result[field, piece(row), :]

    def arrived(field, tile):
        return pltpu.make_async_copy(
            result.at[field, pl.ds(0, 32)],
            outputs[field].at[:, pl.ds(0, 128)],
            out_recv.at[field, tile],
        )

    for field in range(2):
        for tile in range(8):

            @pl.when(jnp.logical_not(here) | (own != tile))
            def _():
                arrived(field, tile).wait()

    for field in range(3):
        for i in range(7):
            moved_in(field, i).wait_send()

        @pl.when(jnp.logical_not(here))
        def _():
            moved_in(field, 7).wait_send()

    for field in range(2):
        for i in range(1, 8):
            moved_out(field, i).wait_send()

        @pl.when(jnp.logical_not(here))
        def _():
            moved_out(field, 0).wait_send()


def body(u_field, v_field, stimulus):
    block = u_field.shape
    state = pltpu.VMEM((4, WIDE, 128), jnp.float32)
    return pl.pallas_call(
        kernel,
        out_shape=[jax.ShapeDtypeStruct(block, jnp.float32)] * 2,
        in_specs=[pl.BlockSpec(memory_space=pl.ANY)] * 3,
        out_specs=[pl.BlockSpec(memory_space=pltpu.VMEM)] * 2,
        scratch_shapes=[
            pltpu.VMEM((3,) + block, jnp.float32),
            pltpu.VMEM((3, 256, STRIP), jnp.float32),
            pltpu.VMEM((6, WIDE, 128), jnp.float32),
            *[state] * 8,
            pltpu.VMEM((2, 256, STRIP), jnp.float32),
            pltpu.SemaphoreType.DMA((3,)),
            pltpu.SemaphoreType.DMA((3, 8)),
            pltpu.SemaphoreType.DMA((3, 8)),
            pltpu.SemaphoreType.DMA((4, 2)),
            pltpu.SemaphoreType.DMA((4, 2)),
            pltpu.SemaphoreType.DMA((2, 8)),
            pltpu.SemaphoreType.DMA((2, 8)),
        ],
        compiler_params=pltpu.CompilerParams(collective_id=0, has_side_effects=True),
    )(u_field, v_field, stimulus)


def solution(mesh):
    return jax.shard_map(
        body,
        mesh=mesh,
        in_specs=(P("row", "col"), P("row", "col"), P("row", "col")),
        out_specs=(P("row", "col"), P("row", "col")),
        check_vma=False,
    )
```

time: 191 us -> 37.9 us (0.20)
  the two profiles are of different devices: /device:TPU:0 before, /device:TPU:4 now
where the time goes in v1:
time: 37.9 us; the launch traced here: 37.7 us
  Pallas kernels  34.8 us (92%)
  local copies, waits for them, and re-layouts  2.26 us (6%)
  between operations  0.65 us (2%)
    pallas_call x1, Pallas kernels, body(): pl.pallas_call(kernel, out_shape=[jax.ShapeDtypeStruct(block, jnp.float32...  34.8 us
    unnamed x4, local copies, waits for them, and re-layouts  2.26 us

profile of v1, /device:TPU:4, one launch (start us, length us, event | category | flops | bytes accessed | tf_op | source)
XLA Modules:
  0.0 37.7 jit_solution(17387261724524827690)
XLA Ops:
  0.6 34.8 %shard_map.50 = (f32[32,1024]{1,0:T(8,128)}, f32[32,1024]{1,0:T(8,128)}) custom-call(f32[32,1024]{1,0:T(8,128)} %u_in.1, f32[32,1024]{1,0:T(8,128)} %v_in.1, f32[32,1024]{1,0:T(8,128)} %s_in.1), custom_call_target="tpu_custom_call" | custom-call | tf_op jit(solution)/shard_map/pallas_call | solution.py:283
  35.5 0.0 copy-start
  35.5 1.6 %copy.7 = f32[32,1024]{1,0:T(8,128)} copy(f32[32,1024]{1,0:T(8,128)} %get-tuple-element.4) | data formatting | bytes 262144
  37.1 0.0 copy-done
  37.1 0.7 %copy.8 = f32[32,1024]{1,0:T(8,128)} copy(f32[32,1024]{1,0:T(8,128)S(1)} %copy-done) | data formatting | bytes 262144
Async XLA Ops:
  35.5 1.6 %copy-start = (f32[32,1024]{1,0:T(8,128)S(1)}, f32[32,1024]{1,0:T(8,128)}, u32[]{:S(2)}) copy-start(f32[32,1024]{1,0:T(8,128)} %get-tuple-element.5) | copy-start | bytes 393220

commit v2 on v1

--- a/solution.py
+++ b/solution.py
@@ -27,8 +27,8 @@
 def place(chip, core):
     group, spot = lax.div(chip, 8), lax.rem(chip, 8)
     half = lax.div(spot, 4)
-    y = half * (7 - spot) + (1 - half) * spot
-    x = lax.rem(half + lax.div(group, 4) + lax.rem(group, 4), 2)
+    y = half * (spot - 4) + (1 - half) * (3 - spot)
+    x = lax.rem(half + lax.div(group, 4) + lax.rem(group, 4) + 1, 2)
     return (2 * y + x, 2 * group + core)
 
 
@@ -74,11 +74,11 @@
     row, col = lax.axis_index("row"), lax.axis_index("col")
     y, x = lax.div(row, 2), lax.rem(row, 2)
     group, core = lax.div(col, 2), lax.rem(col, 2)
-    turned = lax.rem(lax.div(group, 4) + lax.rem(group, 4), 2)
+    turned = lax.rem(lax.div(group, 4) + lax.rem(group, 4) + 1, 2)
     half = lax.rem(x + turned, 2)
-    spot = half * (7 - y) + (1 - half) * y
+    spot = half * (4 + y) + (1 - half) * (3 - y)
     chip = 8 * group + spot
-    own = half * (6 - 2 * y) + (1 - half) * 2 * y + core
+    own = half * 2 * y + (1 - half) * (6 - 2 * y) + core
     here = half == core
     across = lax.rem(core + turned, 2)
 
@@ -95,7 +95,7 @@
     def target(i):
         to_y = lax.rem(y + (2, 1, 3, 0)[i // 2], 4)
         to_core = lax.rem(core + 1 + i, 2)
-        tile = core * (6 - 2 * to_y) + (1 - core) * 2 * to_y + to_core
+        tile = core * 2 * to_y + (1 - core) * (6 - 2 * to_y) + to_core
         return (2 * to_y + across, 2 * group + to_core), tile
 
     def source(i):
@@ -231,9 +231,9 @@
         for parity in range(2):
             block = last[2 * field + parity, HALO : HALO + STRIP, :]
             if field == 0:
-                block = block * SCALE
+                pass
             else:
-                block = block * (SCALE / 0.4) + SHIFT
+                pass
             result[field, pl.ds(parity, 128, stride=2), :] = block.T
         for i in range(1, 8):
             moved_out(field, i).start()
@@ -280,10 +280,10 @@
 def body(u_field, v_field, stimulus):
     block = u_field.shape
     state = pltpu.VMEM((4, WIDE, 128), jnp.float32)
-    return pl.pallas_call(
+    u, v = pl.pallas_call(
         kernel,
         out_shape=[jax.ShapeDtypeStruct(block, jnp.float32)] * 2,
-        in_specs=[pl.BlockSpec(memory_space=pl.ANY)] * 3,
+        in_specs=[pl.BlockSpec(memory_space=pltpu.HBM)] * 3,
         out_specs=[pl.BlockSpec(memory_space=pltpu.VMEM)] * 2,
         scratch_shapes=[
             pltpu.VMEM((3,) + block, jnp.float32),
@@ -299,8 +299,9 @@
             pltpu.SemaphoreType.DMA((2, 8)),
             pltpu.SemaphoreType.DMA((2, 8)),
         ],
-        compiler_params=pltpu.CompilerParams(collective_id=0, has_side_effects=True),
-    )(u_field, v_field, stimulus)
+        compiler_params=pltpu.CompilerParams(collective_id=0, has_side_effects=True, vmem_limit_bytes=12*1024*1024),
+    )(*(pltpu.with_memory_space_constraint(a, pltpu.HBM) for a in (u_field, v_field, stimulus)))
+    return u * SCALE, v * (SCALE / 0.4) + SHIFT
 
 
 def solution(mesh):

time: 37.9 us -> 36.3 us (0.958)
  the two profiles are of different devices: /device:TPU:4 before, /device:TPU:0 now
where the time goes in v2:
time: 36.3 us; the launch traced here: 36.2 us
  Pallas kernels  34.8 us (96%)
  other arithmetic  0.73 us (2%)
  between operations  0.64 us (2%)
    pallas_call x1, Pallas kernels, body(): pl.pallas_call(kernel, out_shape=[jax.ShapeDtypeStruct(block, jnp.float32...  34.8 us
    add x1, other arithmetic, body(): return (u * SCALE, v * (SCALE / 0.4) + SHIFT)  0.73 us

profile of v2, /device:TPU:0, one launch (start us, length us, event | category | flops | bytes accessed | tf_op | source)
XLA Modules:
  0.0 36.2 jit_solution(17195433009250982616)
XLA Ops:
  0.6 34.8 %shard_map.50 = (f32[32,1024]{1,0:T(8,128)S(1)}, f32[32,1024]{1,0:T(8,128)S(1)}) custom-call(f32[32,1024]{1,0:T(8,128)} %u_in.1, f32[32,1024]{1,0:T(8,128)} %v_in.1, f32[32,1024]{1,0:T(8,128)} %s_in.1), custom_call_target="tpu_custom_call" | custom-call | tf_op jit(solution)/shard_map/pallas_call | solution.py:283
  35.4 0.7 %multiply_add_fusion = (f32[32,1024]{1,0:T(8,128)}, f32[32,1024]{1,0:T(8,128)}) fusion(f32[32,1024]{1,0:T(8,128)S(1)} %get-tuple-element.5, f32[32,1024]{1,0:T(8,128)S(1)} %get-tuple-element.4), kind=kLoop, calls=%fused_computation | loop fusion | flops 98304 | bytes 524288 | tf_op jit(solution)/shard_map/add | solution.py:304

commit v3 on v2

v3 whole, which is shorter than its diff:
```python
import jax
import jax.numpy as jnp
from jax import lax
from jax.experimental import pallas as pl
from jax.experimental.pallas import tpu as pltpu
from jax.sharding import PartitionSpec as P

MESH = pl.DeviceIdType.MESH

MICRO_COUNT = 4
MIDDLE = 3
TOP = 3
OUTER = 2

SCALE = 7.5**0.5
SHIFT = 0.875
KEEP_U = 4.4
KEEP_V = 3.9744
COUPLE = 0.0128

STRIP = 128
HALO = 40
ORDER = (0, 1, 2, 3, 4, 5, 6, 7)
BLOCK = 16
STEPS = TOP * MIDDLE * MICRO_COUNT
WIDE = STRIP + 2 * HALO


def place(chip, core):
    group, spot = lax.div(chip, 8), lax.rem(chip, 8)
    upper = lax.div(group, 4)
    level = lax.div(spot, 2)
    back = lax.rem(group, 2)
    y = back * level + (1 - back) * (3 - level)
    x = lax.rem(1 - upper + lax.div(spot + 1, 2), 2)
    return (2 * y + x, 2 * group + core)


def plus(x):
    return pltpu.roll(x, 1, 1)


def minus(x):
    return pltpu.roll(x, 127, 1)


def lanes_summed(pairs, beside, plane, start, rows):
    for i in range(0, len(pairs), 2):
        even, odd = pairs[i], pairs[i + 1]
        beside[plane + i, start : start + rows, :] = odd + plus(odd)
        beside[plane + i + 1, start : start + rows, :] = even + minus(even)


def fine(src, beside, stim, dst, beside_next, low, count, micro, kind, previous, before):
    keep_u, keep_v = KEEP_U, KEEP_V
    if kind > 0:
        keep_u, keep_v = KEEP_U - 4.0, KEEP_V - 4.0
    cube = 1.0 / 64**micro
    rate = 0.125 * 2**kind / 8**micro
    for start in range(low, low + count, BLOCK):
        rows = min(BLOCK, low + count - start)

        def at(ref, plane, shift=0):
            return ref[plane, start + shift : start + shift + rows, :]

        u0, u1, v0, v1 = (at(src, i) for i in range(4))
        total = []
        for i in range(4):
            column = at(src, i, -1) + at(src, i, 1)
            total.append(column + at(beside, i))
        s0, s1 = at(stim, 2 * micro), at(stim, 2 * micro + 1)

        def bent(u):
            square = u * u
            return u * (keep_u - (square if micro == 0 else cube * square))

        new = [
            (total[0] + bent(u0)) + (s0 - v0),
            (total[1] + bent(u1)) + (s1 - v1),
            total[2] + (keep_v * v0 + COUPLE * u0),
            total[3] + (keep_v * v1 + COUPLE * u1),
        ]
        for i in range(4):
            if micro == MICRO_COUNT - 1:
                new[i] = rate * new[i]
            if kind == 2:
                new[i] = new[i] - at(previous, i)
            if kind == 3:
                twice = at(previous, i)
                new[i] = new[i] - (twice + twice) - at(before, i)
            dst[i, start : start + rows, :] = new[i]
        if beside_next is not None:
            lanes_summed(new, beside_next, 0, start, rows)


def kernel(
    u_in, v_in, s_in, u_out, v_out,
    loaded, rows, first, second, ping, pong, t_one, t_two, y_one, y_two, last,
    beside_one, beside_two, drive, result,
    load_sem, in_send, in_recv, halo_send, halo_recv, out_send, out_recv,
):
    row, col = lax.axis_index("row"), lax.axis_index("col")
    y, x = lax.div(row, 2), lax.rem(row, 2)
    group, core = lax.div(col, 2), lax.rem(col, 2)
    back = lax.rem(group, 2)
    level = back * y + (1 - back) * (3 - y)
    side = lax.rem(x + 1 - lax.div(group, 4), 2)
    spot = 2 * level + lax.rem(side + level, 2)
    half = lax.div(spot, 4)
    chip = 8 * group + spot
    own = 2 * (spot - 4 * half) + core
    here = half == core

    inputs = (u_in, v_in, s_in)
    loads = [
        pltpu.make_async_copy(inputs[i], loaded.at[i], load_sem.at[i]) for i in range(3)
    ]
    for load in loads:
        load.start()

    left = place(lax.rem(chip + 63 + core, 64), 1 - core)
    right = place(lax.rem(chip + core, 64), 1 - core)

    def target(i):
        tile = lax.rem(own + 1 + i, 8)
        return place(8 * group + 4 * core + lax.div(tile, 2), lax.rem(tile, 2)), tile

    def source(i):
        return lax.rem(row + i, 8)

    barrier = pltpu.get_barrier_semaphore()

    def greet(device):
        pl.semaphore_signal(barrier, inc=1, device_id=device, device_id_type=MESH)

    for i in range(7):
        greet(target(i)[0])
        greet((source(i + 1), 2 * group + half))

    @pl.when(jnp.logical_not(here))
    def _():
        greet(target(7)[0])
        greet((source(0), 2 * group + half))

    greet(left)
    greet(right)
    pl.semaphore_wait(barrier, 16 + 2 * (1 - jnp.where(here, 1, 0)))

    def lanes(tile):
        return pl.ds(pl.multiple_of(tile * 128, 128), 128)

    def piece(where):
        return pl.ds(pl.multiple_of(where * 32, 32), 32)

    def moved_in(field, i):
        device, tile = target(i)
        return pltpu.make_async_remote_copy(
            src_ref=loaded.at[field, :, lanes(tile)],
            dst_ref=rows.at[field, piece(row)],
            send_sem=in_send,
            recv_sem=in_recv.at[field],
            device_id=device,
            device_id_type=MESH,
        )

    def kept_in(field):
        return pltpu.make_async_copy(
            inputs[field].at[:, lanes(own)], rows.at[field, piece(row)], in_recv.at[field]
        )

    for field in range(3):
        loads[field].wait()
        for i in range(7):
            moved_in(field, i).start()

        @pl.when(here)
        def _():
            kept_in(field).start()

        @pl.when(jnp.logical_not(here))
        def _():
            moved_in(field, 7).start()

    def edge(buffer, planes, which, side):
        mine, theirs = ((HALO, WIDE - HALO), (WIDE - 2 * HALO, 0))[side]
        return pltpu.make_async_remote_copy(
            src_ref=buffer.at[planes, pl.ds(mine, HALO)],
            dst_ref=buffer.at[planes, pl.ds(theirs, HALO)],
            send_sem=halo_send.at[which, side],
            recv_sem=halo_recv.at[which, side],
            device_id=(left, right)[side],
            device_id_type=MESH,
        )

    edges = []
    for field in range(3):
        pltpu.make_async_copy(rows.at[field], rows.at[field], in_recv.at[field]).wait()
        for parity in range(2):
            block = rows[field, pl.ds(parity, 128, stride=2), :].T
            if field == 0:
                block = block * (1.0 / SCALE)
            else:
                block = (block - SHIFT) * (0.4 / SCALE)
            first[2 * field + parity, HALO : HALO + STRIP, :] = block
        for side in range(2):
            copy = edge(first, pl.ds(2 * field, 2), field, side)
            copy.start()
            edges.append(copy)
        if field < 2:
            pair = [first[2 * field + parity, HALO : HALO + STRIP, :] for parity in range(2)]
            lanes_summed(pair, beside_one, 2 * field, HALO, STRIP)

    def halos_summed(state):
        @pl.when(row >= 0)
        def _():
            for low in (0, HALO + STRIP):
                planes = [state[i, low : low + HALO, :] for i in range(4)]
                lanes_summed(planes, beside_one, 0, low, HALO)

    for copy in edges:
        copy.wait()
    for micro in range(MICRO_COUNT):
        for parity in range(2):
            drive[2 * micro + parity, :, :] = 8.0**micro * first[4 + parity, :, :]

    halos_summed(first)
    start = first
    for outer in range(OUTER):
        done = 0
        state = start
        goal = (second, last)[outer]
        for top in range(TOP):
            for middle in range(MIDDLE):
                end = (t_one, t_two, (y_one, y_two, goal)[top])[middle]
                for micro in range(MICRO_COUNT):
                    done += 1
                    low = HALO - STEPS + done
                    count = -(-(WIDE - 2 * low) // 8) * 8
                    ends = micro == MICRO_COUNT - 1
                    kind = 0
                    if ends:
                        kind = 1 + (middle == MIDDLE - 1) * (1 + (top == TOP - 1))
                    into = end if ends else (ping, pong)[micro % 2]
                    beside = (beside_two, beside_one)[done % 2]
                    beside_next = (beside_one, beside_two)[done % 2]
                    if done == STEPS and outer == OUTER - 1:
                        beside_next = None
                    fine(
                        state, beside, drive, into, beside_next,
                        low, count, micro, kind, t_two, y_two,
                    )
                    state = into
        start = goal
        if outer < OUTER - 1:
            edges = [edge(second, pl.ds(0, 4), 3 + outer, side) for side in range(2)]
            for copy in edges:
                copy.start()
            for copy in edges:
                copy.wait()
            halos_summed(second)

    outputs = (u_out, v_out)

    def moved_out(field, to):
        return pltpu.make_async_remote_copy(
            src_ref=result.at[field, pl.ds(32 * to, 32)],
            dst_ref=outputs[field].at[:, lanes(own)],
            send_sem=out_send,
            recv_sem=out_recv,
            device_id=(jnp.int32(to), 2 * group + half),
            device_id_type=MESH,
        )

    for field in range(2):
        for parity in range(2):
            block = last[2 * field + parity, HALO : HALO + STRIP, :]
            result[field, pl.ds(parity, 128, stride=2), :] = block.T
    for to in ORDER:

        @pl.when(jnp.logical_not(here) | (row != to))
        def _():
            moved_out(0, to).start()
            moved_out(1, to).start()

    @pl.when(here)
    def _():
        for field in range(2):
            outputs[field][:, lanes(own)] = result[field, piece(row), :]

    def settle(count):
        for buffer, semaphore in ((result, out_recv), (rows, in_send), (result, out_send)):
            part = buffer.at[:, pl.ds(0, 32 * count)]
            pltpu.make_async_copy(part, part, semaphore).wait()

    @pl.when(here)
    def _():
        settle(7)

    @pl.when(jnp.logical_not(here))
    def _():
        settle(8)


def body(u_field, v_field, stimulus):
    block = u_field.shape
    state = pltpu.VMEM((4, WIDE, 128), jnp.float32)
    u, v = pl.pallas_call(
        kernel,
        out_shape=[jax.ShapeDtypeStruct(block, jnp.float32)] * 2,
        in_specs=[pl.BlockSpec(memory_space=pltpu.HBM)] * 3,
        out_specs=[pl.BlockSpec(memory_space=pltpu.VMEM)] * 2,
        scratch_shapes=[
            pltpu.VMEM((3,) + block, jnp.float32),
            pltpu.VMEM((3, 256, STRIP), jnp.float32),
            pltpu.VMEM((6, WIDE, 128), jnp.float32),
            *[state] * 10,
            pltpu.VMEM((2 * MICRO_COUNT, WIDE, 128), jnp.float32),
            pltpu.VMEM((2, 256, STRIP), jnp.float32),
            pltpu.SemaphoreType.DMA((3,)),
            pltpu.SemaphoreType.DMA,
            pltpu.SemaphoreType.DMA((3,)),
            pltpu.SemaphoreType.DMA((4, 2)),
            pltpu.SemaphoreType.DMA((4, 2)),
            pltpu.SemaphoreType.DMA,
            pltpu.SemaphoreType.DMA,
        ],
        compiler_params=pltpu.CompilerParams(collective_id=0, has_side_effects=True, vmem_limit_bytes=12*1024*1024),
    )(*(pltpu.with_memory_space_constraint(a, pltpu.HBM) for a in (u_field, v_field, stimulus)))
    return u * SCALE, v * (SCALE / 0.4) + SHIFT


def solution(mesh):
    return jax.shard_map(
        body,
        mesh=mesh,
        in_specs=(P("row", "col"), P("row", "col"), P("row", "col")),
        out_specs=(P("row", "col"), P("row", "col")),
        check_vma=False,
    )
```

time: 36.3 us -> 34.2 us (0.942)
  Pallas kernels: 34.8 us -> 32.7 us
    pallas_call x1, Pallas kernels: 34.8 us -> 32.7 us  [body(): pl.pallas_call(kernel, out_shape=[jax.ShapeDtypeStruct(block, jnp.float32...]
where the time goes in v3:
time: 34.2 us; the launch traced here: 34.1 us
  Pallas kernels  32.7 us (96%)
  other arithmetic  0.73 us (2%)
  between operations  0.64 us (2%)
    pallas_call x1, Pallas kernels, body(): pl.pallas_call(kernel, out_shape=[jax.ShapeDtypeStruct(block, jnp.float32...  32.7 us
    add x1, other arithmetic, body(): return (u * SCALE, v * (SCALE / 0.4) + SHIFT)  0.73 us

profile of v3, /device:TPU:0, one launch (start us, length us, event | category | flops | bytes accessed | tf_op | source)
XLA Modules:
  0.0 34.1 jit_solution(8732088722584158361)
XLA Ops:
  0.6 32.7 %shard_map.50 = (f32[32,1024]{1,0:T(8,128)S(1)}, f32[32,1024]{1,0:T(8,128)S(1)}) custom-call(f32[32,1024]{1,0:T(8,128)} %u_in.1, f32[32,1024]{1,0:T(8,128)} %v_in.1, f32[32,1024]{1,0:T(8,128)} %s_in.1), custom_call_target="tpu_custom_call" | custom-call | tf_op jit(solution)/shard_map/pallas_call | solution.py:307
  33.4 0.7 %multiply_add_fusion = (f32[32,1024]{1,0:T(8,128)}, f32[32,1024]{1,0:T(8,128)}) fusion(f32[32,1024]{1,0:T(8,128)S(1)} %get-tuple-element.5, f32[32,1024]{1,0:T(8,128)S(1)} %get-tuple-element.4), kind=kLoop, calls=%fused_computation | loop fusion | flops 98304 | bytes 524288 | tf_op jit(solution)/shard_map/add | solution.py:329

commit v4 on v3

--- a/solution.py
+++ b/solution.py
@@ -26,14 +26,18 @@
 WIDE = STRIP + 2 * HALO
 
 
-def place(chip, core):
+def swapped(group):
+    return 1 - lax.div(lax.rem(group, 4), 2)
+
+
+def place(chip, side):
     group, spot = lax.div(chip, 8), lax.rem(chip, 8)
     upper = lax.div(group, 4)
     level = lax.div(spot, 2)
     back = lax.rem(group, 2)
     y = back * level + (1 - back) * (3 - level)
     x = lax.rem(1 - upper + lax.div(spot + 1, 2), 2)
-    return (2 * y + x, 2 * group + core)
+    return (2 * y + x, 2 * group + lax.rem(side + swapped(group), 2))
 
 
 def plus(x):
@@ -108,7 +112,8 @@
     spot = 2 * level + lax.rem(side + level, 2)
     half = lax.div(spot, 4)
     chip = 8 * group + spot
-    own = 2 * (spot - 4 * half) + core
+    hand = lax.rem(core + swapped(group), 2)
+    own = 2 * (spot - 4 * half) + hand
     here = half == core
 
     inputs = (u_in, v_in, s_in)
@@ -118,8 +123,8 @@
     for load in loads:
         load.start()
 
-    left = place(lax.rem(chip + 63 + core, 64), 1 - core)
-    right = place(lax.rem(chip + core, 64), 1 - core)
+    left = place(lax.rem(chip + 63 + hand, 64), 1 - hand)
+    right = place(lax.rem(chip + hand, 64), 1 - hand)
 
     def target(i):
         tile = lax.rem(own + 1 + i, 8)
@@ -133,18 +138,19 @@
     def greet(device):
         pl.semaphore_signal(barrier, inc=1, device_id=device, device_id_type=MESH)
 
-    for i in range(7):
-        greet(target(i)[0])
-        greet((source(i + 1), 2 * group + half))
+    for i in range(1, 8):
+        greet((source(i), 2 * group + half))
 
     @pl.when(jnp.logical_not(here))
     def _():
-        greet(target(7)[0])
-        greet((source(0), 2 * group + half))
-
+        greet((row, 2 * group + half))
+
+    for i in range(4):
+        to_row = place(8 * group + 4 * core + i, 0)[0]
+        greet((to_row, 2 * group + 1 - half))
     greet(left)
     greet(right)
-    pl.semaphore_wait(barrier, 16 + 2 * (1 - jnp.where(here, 1, 0)))
+    pl.semaphore_wait(barrier, 14 - jnp.where(here, 1, 0))
 
     def lanes(tile):
         return pl.ds(pl.multiple_of(tile * 128, 128), 128)

time: 34.2 us -> 32.9 us (0.962)
  Pallas kernels: 32.7 us -> 31.4 us
    pallas_call x1, Pallas kernels: 32.7 us -> 31.4 us  [body(): pl.pallas_call(kernel, out_shape=[jax.ShapeDtypeStruct(block, jnp.float32...]
where the time goes in v4:
time: 32.9 us; the launch traced here: 32.8 us
  Pallas kernels  31.4 us (95%)
  other arithmetic  0.73 us (2%)
  between operations  0.64 us (2%)
    pallas_call x1, Pallas kernels, body(): pl.pallas_call(kernel, out_shape=[jax.ShapeDtypeStruct(block, jnp.float32...  31.4 us
    add x1, other arithmetic, body(): return (u * SCALE, v * (SCALE / 0.4) + SHIFT)  0.73 us

profile of v4, /device:TPU:0, one launch (start us, length us, event | category | flops | bytes accessed | tf_op | source)
XLA Modules:
  0.0 32.8 jit_solution(17327463519860494577)
XLA Ops:
  0.6 31.4 %shard_map.50 = (f32[32,1024]{1,0:T(8,128)S(1)}, f32[32,1024]{1,0:T(8,128)S(1)}) custom-call(f32[32,1024]{1,0:T(8,128)} %u_in.1, f32[32,1024]{1,0:T(8,128)} %v_in.1, f32[32,1024]{1,0:T(8,128)} %s_in.1), custom_call_target="tpu_custom_call" | custom-call | tf_op jit(solution)/shard_map/pallas_call | solution.py:313
  32.0 0.7 %multiply_add_fusion = (f32[32,1024]{1,0:T(8,128)}, f32[32,1024]{1,0:T(8,128)}) fusion(f32[32,1024]{1,0:T(8,128)S(1)} %get-tuple-element.5, f32[32,1024]{1,0:T(8,128)S(1)} %get-tuple-element.4), kind=kLoop, calls=%fused_computation | loop fusion | flops 98304 | bytes 524288 | tf_op jit(solution)/shard_map/add | solution.py:335

commit v5 on v4

--- a/solution.py
+++ b/solution.py
@@ -24,6 +24,7 @@
 BLOCK = 16
 STEPS = TOP * MIDDLE * MICRO_COUNT
 WIDE = STRIP + 2 * HALO
+PLANE = WIDE + 8
 
 
 def swapped(group):
@@ -192,13 +193,21 @@
         return pltpu.make_async_remote_copy(
             src_ref=buffer.at[planes, pl.ds(mine, HALO)],
             dst_ref=buffer.at[planes, pl.ds(theirs, HALO)],
-            send_sem=halo_send.at[which, side],
-            recv_sem=halo_recv.at[which, side],
+            send_sem=halo_send.at[which],
+            recv_sem=halo_recv.at[which],
             device_id=(left, right)[side],
             device_id_type=MESH,
         )
 
-    edges = []
+    def driven(low, count):
+        for micro in range(MICRO_COUNT):
+            for parity in range(2):
+                value = first[4 + parity, low : low + count, :]
+                drive[2 * micro + parity, low : low + count, :] = 8.0**micro * value
+
+    def edges_of(buffer):
+        return buffer.at[:, pl.ds(0, 2 * HALO)]
+
     for field in range(3):
         pltpu.make_async_copy(rows.at[field], rows.at[field], in_recv.at[field]).wait()
         for parity in range(2):
@@ -209,12 +218,12 @@
                 block = (block - SHIFT) * (0.4 / SCALE)
             first[2 * field + parity, HALO : HALO + STRIP, :] = block
         for side in range(2):
-            copy = edge(first, pl.ds(2 * field, 2), field, side)
-            copy.start()
-            edges.append(copy)
+            edge(first, pl.ds(2 * field, 2), 0, side).start()
         if field < 2:
             pair = [first[2 * field + parity, HALO : HALO + STRIP, :] for parity in range(2)]
             lanes_summed(pair, beside_one, 2 * field, HALO, STRIP)
+        else:
+            driven(HALO, STRIP)
 
     def halos_summed(state):
         @pl.when(row >= 0)
@@ -223,12 +232,9 @@
                 planes = [state[i, low : low + HALO, :] for i in range(4)]
                 lanes_summed(planes, beside_one, 0, low, HALO)
 
-    for copy in edges:
-        copy.wait()
-    for micro in range(MICRO_COUNT):
-        for parity in range(2):
-            drive[2 * micro + parity, :, :] = 8.0**micro * first[4 + parity, :, :]
-
+    pltpu.make_async_copy(edges_of(first), edges_of(first), halo_recv.at[0]).wait()
+    driven(0, HALO)
+    driven(HALO + STRIP, HALO)
     halos_summed(first)
     start = first
     for outer in range(OUTER):
@@ -258,11 +264,9 @@
                     state = into
         start = goal
         if outer < OUTER - 1:
-            edges = [edge(second, pl.ds(0, 4), 3 + outer, side) for side in range(2)]
-            for copy in edges:
-                copy.start()
-            for copy in edges:
-                copy.wait()
+            for side in range(2):
+                edge(second, pl.ds(0, 4), 1, side).start()
+            pltpu.make_async_copy(edges_of(second), edges_of(second), halo_recv.at[1]).wait()
             halos_summed(second)
 
     outputs = (u_out, v_out)
@@ -298,6 +302,9 @@
             part = buffer.at[:, pl.ds(0, 32 * count)]
             pltpu.make_async_copy(part, part, semaphore).wait()
 
+    pltpu.make_async_copy(edges_of(first), edges_of(first), halo_send.at[0]).wait()
+    pltpu.make_async_copy(edges_of(second), edges_of(second), halo_send.at[1]).wait()
+
     @pl.when(here)
     def _():
         settle(7)
@@ -309,7 +316,7 @@
 
 def body(u_field, v_field, stimulus):
     block = u_field.shape
-    state = pltpu.VMEM((4, WIDE, 128), jnp.float32)
+    state = pltpu.VMEM((4, PLANE, 128), jnp.float32)
     u, v = pl.pallas_call(
         kernel,
         out_shape=[jax.ShapeDtypeStruct(block, jnp.float32)] * 2,
@@ -318,15 +325,15 @@
         scratch_shapes=[
             pltpu.VMEM((3,) + block, jnp.float32),
             pltpu.VMEM((3, 256, STRIP), jnp.float32),
-            pltpu.VMEM((6, WIDE, 128), jnp.float32),
+            pltpu.VMEM((6, PLANE, 128), jnp.float32),
             *[state] * 10,
-            pltpu.VMEM((2 * MICRO_COUNT, WIDE, 128), jnp.float32),
+            pltpu.VMEM((2 * MICRO_COUNT, PLANE, 128), jnp.float32),
             pltpu.VMEM((2, 256, STRIP), jnp.float32),
             pltpu.SemaphoreType.DMA((3,)),
             pltpu.SemaphoreType.DMA,
             pltpu.SemaphoreType.DMA((3,)),
-            pltpu.SemaphoreType.DMA((4, 2)),
-            pltpu.SemaphoreType.DMA((4, 2)),
+            pltpu.SemaphoreType.DMA((2,)),
+            pltpu.SemaphoreType.DMA((2,)),
             pltpu.SemaphoreType.DMA,
             pltpu.SemaphoreType.DMA,
         ],

time: 32.9 us -> 32.7 us (level)
  no operation moved by 1% of the time
where the time goes in v5:
time: 32.7 us; the launch traced here: 32.6 us
  Pallas kernels  31.2 us (95%)
  other arithmetic  0.73 us (2%)
  between operations  0.64 us (2%)
    pallas_call x1, Pallas kernels, body(): pl.pallas_call(kernel, out_shape=[jax.ShapeDtypeStruct(block, jnp.float32...  31.2 us
    add x1, other arithmetic, body(): return (u * SCALE, v * (SCALE / 0.4) + SHIFT)  0.73 us

profile of v5, /device:TPU:0, one launch (start us, length us, event | category | flops | bytes accessed | tf_op | source)
XLA Modules:
  0.0 32.6 jit_solution(11906633805031511020)
XLA Ops:
  0.6 31.2 %shard_map.50 = (f32[32,1024]{1,0:T(8,128)S(1)}, f32[32,1024]{1,0:T(8,128)S(1)}) custom-call(f32[32,1024]{1,0:T(8,128)} %u_in.1, f32[32,1024]{1,0:T(8,128)} %v_in.1, f32[32,1024]{1,0:T(8,128)} %s_in.1), custom_call_target="tpu_custom_call" | custom-call | tf_op jit(solution)/shard_map/pallas_call | solution.py:320
  31.9 0.7 %multiply_add_fusion = (f32[32,1024]{1,0:T(8,128)}, f32[32,1024]{1,0:T(8,128)}) fusion(f32[32,1024]{1,0:T(8,128)S(1)} %get-tuple-element.5, f32[32,1024]{1,0:T(8,128)S(1)} %get-tuple-element.4), kind=kLoop, calls=%fused_computation | loop fusion | flops 98304 | bytes 524288 | tf_op jit(solution)/shard_map/add | solution.py:342
